TPU v7x, 128 devices: a whole 4x4x4 slice. The times are simulated.
128 devices in a mesh: seq: 16 (over x_lo, z, core), head: 4 (over y), batch: 2 (over x_hi).
Axes of the slice: x: 4 (x_hi: 2, x_lo: 2; x = x_hi * 2 + x_lo), y: 4, z: 4, core: 2. Of those that a mesh axis runs over, the one named last changes fastest.
Arguments:
- tokens: bfloat16 [32768, 2048], P(('batch', 'seq')), parts along dimension 0, may hold values from -6 to 6
- neighbor_bank: bfloat16 [512, 256, 2048], P(('batch', 'seq')), parts along dimension 0, may hold values from -2100 to 2100
- slots: int32 [512], P(('batch', 'seq')), parts along dimension 0, may hold values from 0 to 15
- w_query: bfloat16 [2048, 2048], P('seq', 'head'), may hold values from -0.125 to 0.125
- w_key: bfloat16 [2048, 2048], P('seq', 'head'), may hold values from -0.125 to 0.125
- w_value: bfloat16 [2048, 2048], P('seq', 'head'), may hold values from -0.125 to 0.125
- w_out: bfloat16 [2048, 2048], P('head', 'seq'), may hold values from -0.125 to 0.125
Outputs:
- cross_out: bfloat16 [32768, 2048], P(('batch', 'seq'), 'head'), parts along dimension 0
There are 2 independent parts, one for each index of `batch`. A program takes and returns all parts, laid end to end along the dimension named above; an argument that names none is the same for every part. Nothing has to cross between parts.
Inputs may be any that keep to these rules, and one draw needn't show every extreme that they name: Entry c picks row c // 16 * 16 + slots[c] of neighbor_bank.
All inputs are finite; a program needn't handle non-finite values.
Results may differ from a plain program's by a relative error of at most 0.006.
The roundings to bfloat16 on the way count: a program that leaves them out, or rounds other values in their place, can miss the bound.
Values may be sent and summed in bfloat16 or wider, within the bound.
No kernel may reach another device: no remote copies, remote signals or barrier semaphores. Data moves between devices by JAX's collectives and lax.ppermute only.
A program may use at most 128 MiB of HBM per device.

v0:
```python
import math
import jax
import jax.numpy as jnp
from jax import lax
from jax.sharding import PartitionSpec as P

HEAD_DIM = 128


def passed_along(block, axis, distance):
    devices = range(lax.axis_size(axis))
    route = [(i - distance, i) for i in devices if i - distance in devices]
    return lax.ppermute(block, axis, route)


def side_by_side(arrays, axis, dim, along):
    ends, at = ([], 0)
    for a in arrays[:-1]:
        at += a.shape[along]
        ends.append(at)
    both = jnp.concatenate(arrays, axis=along)
    return tuple(jnp.split(lax.all_gather(both, axis, axis=dim, tiled=True), ends, axis=along))


def attend(query_blocks, key_blocks, value_blocks):
    scores = jnp.einsum(
        "cmhd,cnhd->chmn", query_blocks, key_blocks, preferred_element_type=jnp.float32
    ) / math.sqrt(HEAD_DIM)
    peak_score = jnp.max(scores, axis=-1, keepdims=True)
    exponent = jnp.exp(scores - peak_score)
    weights = (exponent / jnp.sum(exponent, axis=-1, keepdims=True)).astype(jnp.bfloat16)
    blended = jnp.einsum(
        "chmn,cnhd->cmhd", weights, value_blocks, preferred_element_type=jnp.float32
    ).astype(jnp.bfloat16)
    return blended.reshape(blended.shape[0] * blended.shape[1], blended.shape[2] * blended.shape[3])


def fold_rows(source, shard_rows):
    return jnp.dot(source, shard_rows, preferred_element_type=jnp.float32)


def local(tokens, neighbor_bank, slots, w_query, w_key, w_value, w_out):
    tok_rows, model_width = tokens.shape
    block_count = neighbor_bank.shape[0]
    neighbor_rows = neighbor_bank.shape[1]
    block_len = tok_rows // block_count
    local_width = w_query.shape[1]
    local_heads = local_width // HEAD_DIM
    hidden = tokens.astype(jnp.float32)
    normed = (hidden * lax.rsqrt(jnp.mean(hidden * hidden, axis=-1, keepdims=True) + 1e-06)).astype(
        jnp.bfloat16
    )
    retrieved = jnp.take(neighbor_bank, slots, axis=0)
    arrived = passed_along(retrieved[block_count - 1], "seq", 1)
    context = jnp.concatenate([arrived[None], retrieved[: block_count - 1]], axis=0)
    context_flat = context.reshape(block_count * neighbor_rows, model_width)
    shard_rows = side_by_side((w_query, w_key, w_value), "seq", 0, 1)
    query_sum = fold_rows(normed, shard_rows[0])
    key_sum = fold_rows(context_flat, shard_rows[1])
    value_sum = fold_rows(context_flat, shard_rows[2])
    query_blocks = query_sum.astype(jnp.bfloat16).reshape(
        block_count, block_len, local_heads, HEAD_DIM
    )
    key_blocks = key_sum.astype(jnp.bfloat16).reshape(
        block_count, neighbor_rows, local_heads, HEAD_DIM
    )
    value_blocks = value_sum.astype(jnp.bfloat16).reshape(
        block_count, neighbor_rows, local_heads, HEAD_DIM
    )
    attended = attend(query_blocks, key_blocks, value_blocks)
    every_head = lax.all_gather(attended, "head", axis=1, tiled=True)
    wide_rows = lax.all_gather(w_out, "seq", axis=1, tiled=True)
    own_columns = lax.all_to_all(wide_rows, "head", split_axis=1, concat_axis=0, tiled=True)
    return jnp.dot(every_head, own_columns, preferred_element_type=jnp.float32).astype(jnp.bfloat16)


def solution(mesh):
    in_specs = (
        P(("batch", "seq"), None),
        P(("batch", "seq"), None, None),
        P(("batch", "seq")),
        P("seq", "head"),
        P("seq", "head"),
        P("seq", "head"),
        P("head", "seq"),
    )
    out_specs = P(("batch", "seq"), "head")
    return jax.shard_map(local, mesh=mesh, in_specs=in_specs, out_specs=out_specs, check_vma=False)
```

profile of v0, /device:TPU:3, one launch (start us, length us, event | category | flops | bytes accessed | tf_op | source)
XLA Modules:
  0.0 214.9 jit_solution(9233872285534013376)
XLA Ops:
  6.5 1.8 pad_maximum_fusion.1
  8.3 0.0 all-gather.4.cloned.1.call-update
  8.4 0.0 all-gather.8.cloned.1.call-start
  8.4 0.7 compare_select_fusion
  9.1 13.1 %gather_fusion = bf16[16,256,2048]{2,1,0:T(8,128)(2,1)} fusion(bf16[16,256,2048]{2,1,0:T(8,128)(2,1)} %param.8, s32[1024]{0:T(1024)S(1)} %pad_clamp_fusion), kind=kCustom, calls=%fused_computation | custom fusion | bytes 33554496 | tf_op jit(solution)/shard_map/jit(_take)/gather | solution.py:53
  22.2 8.7 %broadcast_select_fusion = bf16[16,256,2048]{2,1,0:T(8,128)(2,1)S(1)} fusion(bf16[16,256,2048]{2,1,0:T(8,128)(2,1)} %gather_fusion, pred[16]{0:T(512)(128)(4,1)S(1)} %compare_and_fusion), kind=kLoop, calls=%fused_computation.3 | loop fusion | flops 8388608 | bytes 33554448 | tf_op jit(solution)/shard_map/jit(_take)/select_n | solution.py:53
  31.0 5.9 %copy-done = bf16[16,256,2048]{2,1,0:T(8,128)(2,1)} copy-done((bf16[16,256,2048]{2,1,0:T(8,128)(2,1)}, bf16[16,256,2048]{2,1,0:T(8,128)(2,1)S(1)}, u32[]{:S(2)}) %copy-start) | copy-done | bytes 16777240
  36.9 0.1 slice_bitcast_fusion
  37.0 4.1 %collective-permute-start = (bf16[256,2048]{1,0:T(8,128)(2,1)S(1)}, bf16[256,2048]{1,0:T(8,128)(2,1)S(1)}, u32[]{:S(2)}, u32[]{:S(2)}) collective-permute-start(bf16[256,2048]{1,0:T(8,128)(2,1)S(1)} %slice_bitcast_fusion), channel_id=1, source_target_pairs={{0,8},{8,16},{16,24},{24,32},{32,40},{40,48},{48,56},{56,64},{64,7... | collective-permute-start | bytes 3145736 | tf_op jit(solution)/shard_map/ppermute | solution.py:13
  41.1 0.8 copy.19
  41.9 0.0 all-gather.6.cloned.1.call-start
  42.0 2.2 %copy-done.1 = bf16[1024,2048]{1,0:T(8,128)(2,1)S(1)} copy-done((bf16[1024,2048]{1,0:T(8,128)(2,1)S(1)}, bf16[1024,2048]{1,0:T(8,128)(2,1)}, u32[]{:S(2)}) %copy-start.1) | copy-done | bytes 4194328
  44.2 0.9 fusion.1
  45.1 16.4 %collective-permute-done = bf16[256,2048]{1,0:T(8,128)(2,1)S(1)} collective-permute-done((bf16[256,2048]{1,0:T(8,128)(2,1)S(1)}, bf16[256,2048]{1,0:T(8,128)(2,1)S(1)}, u32[]{:S(2)}, u32[]{:S(2)}) %collective-permute-start) | collective-permute-done | bytes 1048608 | tf_op jit(solution)/shard_map/ppermute | solution.py:13
  61.5 6.4 %pad_maximum_fusion = bf16[16,256,2048]{2,1,0:T(8,128)(2,1)} fusion(bf16[15,256,2048]{2,1,0:T(8,128)(2,1)S(1)} %slice-done, bf16[1,256,2048]{2,1,0:T(8,128)(2,1)S(1)} %bitcast.25), kind=kLoop, calls=%fused_computation.2 | loop fusion | flops 8388608 | bytes 33554432 | tf_op jit(solution)/shard_map/concatenate | solution.py:55
  68.0 14.5 %convolution_convert_fusion = bf16[4096,512]{1,0:T(8,128)(2,1)} fusion(bf16[4096,2048]{1,0:T(8,128)(2,1)} %bitcast.18, bf16[2048,1536]{1,0:T(8,128)(2,1)} %all-gather.4.cloned.1.call-done), kind=kOutput, calls=%fused_computation.8 | convolution fusion | flops 8592031744 | bytes 23068672 | tf_op jit(solution)/shard_map/dot_general | solution.py:39
  82.4 7.0 %reshape.36 = bf16[16,256,4,128]{3,2,1,0:T(4,128)(2,1)} reshape(bf16[4096,512]{1,0:T(8,128)(2,1)} %convolution_convert_fusion) | data formatting | bytes 8388608 | tf_op jit(solution)/shard_map/reshape | solution.py:64
  89.4 5.2 %fusion.21 = bf16[1024,512]{1,0:T(8,128)(2,1)S(1)} fusion(bf16[2048,1536]{1,0:T(8,128)(2,1)} %all-gather.4.cloned.1.call-done, bf16[1024,2048]{1,0:T(8,128)(2,1)} %param.7, f32[1024]{0:T(1024)S(1)} %add_rsqrt_fusion), kind=kOutput, calls=%fused_computation.26 | convolution fusion | flops 2154299392 | bytes 7344128 | tf_op jit(solution)/shard_map/dot_general | solution.py:39
  94.6 0.3 reshape.35
  94.9 14.4 %convolution_convert_fusion.1 = bf16[4096,512]{1,0:T(8,128)(2,1)} fusion(bf16[4096,2048]{1,0:T(8,128)(2,1)} %bitcast.19, bf16[2048,1536]{1,0:T(8,128)(2,1)} %all-gather.4.cloned.1.call-done), kind=kOutput, calls=%fused_computation.9 | convolution fusion | flops 8592031744 | bytes 23068672 | tf_op jit(solution)/shard_map/dot_general | solution.py:39
  109.3 6.9 %reshape.34 = bf16[16,256,4,128]{3,2,1,0:T(4,128)(2,1)} reshape(bf16[4096,512]{1,0:T(8,128)(2,1)} %convolution_convert_fusion.1) | data formatting | bytes 8388608 | tf_op jit(solution)/shard_map/reshape | solution.py:67
  116.2 3.8 %fusion.7 = f32[16,4,64,256]{3,2,1,0:T(8,128)S(1)} fusion(bf16[16,256,4,128]{3,2,1,0:T(4,128)(2,1)} %reshape.36, bf16[16,64,4,128]{3,2,1,0:T(4,128)(2,1)S(1)} %reshape.35), kind=kOutput, calls=%fused_computation.13 | convolution fusion | flops 268435456 | bytes 9437184 | tf_op jit(solution)/shard_map/cmhd,cnhd->chmn/dot_general | solution.py:26
  120.0 2.0 copy-done.2
  122.0 1.6 fusion.38
  123.6 11.9 %fusion.26 = bf16[16,64,4,128]{3,1,2,0:T(8,128)(2,1)S(1)} fusion(bf16[16,256,4,128]{3,2,1,0:T(4,128)(2,1)} %reshape.34, f32[16,4,64]{2,1,0:T(4,128)S(1)} %fusion.38, f32[16,4,64,256]{3,2,1,0:T(8,128)} %copy-done.2), kind=kOutput, calls=%fused_computation.28 | convolution fusion | flops 274206976 | bytes 9453568 | tf_op jit(solution)/shard_map/chmn,cnhd->cmhd/dot_general | solution.py:32
  135.5 0.9 copy.18
  136.4 1.2 copy.33
  137.6 0.0 all-gather.8.cloned.1.call-done
  137.6 35.9 %all_to_all.19 = bf16[512,4,512]{0,2,1:T(8,128)(2,1)S(1)} all-to-all(bf16[512,4,512]{0,2,1:T(8,128)(2,1)} %bitcast.23), channel_id=1, replica_groups=mesh['seq'=16,'head'=4,'batch'=2] {'head'}, dimensions={1} | all-to-all | bytes 4194304 | tf_op jit(solution)/shard_map/all_to_all | solution.py:73
  173.5 2.4 %copy.20 = bf16[4,512,512]{2,1,0:T(8,128)(2,1)} copy(bf16[4,512,512]{1,2,0:T(8,128)(2,1)S(1)} %bitcast.20) | data formatting | bytes 4194304 | tf_op jit(solution)/shard_map/all_to_all | solution.py:73
  175.9 26.3 %all-gather.6.cloned.1.call-done = bf16[1024,2048]{1,0:T(8,128)(2,1)} async-done(((bf16[1024,512]{1,0:T(8,128)(2,1)}), bf16[1024,2048]{1,0:T(8,128)(2,1)}) %all-gather.6.cloned.1.call-update) | async-done | bytes 4194320 | tf_op jit(solution)/shard_map/all_gather | solution.py:71
  202.2 6.2 %convolution_convert_fusion.2 = bf16[1024,512]{1,0:T(8,128)(2,1)} fusion(bf16[1024,2048]{1,0:T(8,128)(2,1)} %all-gather.6.cloned.1.call-done, bf16[2048,512]{1,0:T(8,128)(2,1)} %bitcast.24), kind=kOutput, calls=%fused_computation.27 | convolution fusion | flops 2148007936 | bytes 7340032 | tf_op jit(solution)/shard_map/dot_general | solution.py:74
  (16 shorter events, 0.1 us)
Async XLA Ops:
  6.5 61.4 %all-gather.4.cloned.1.call-start = ((), (), s32[]{:S(2)}) async-start(), calls=%async_computation.1 | async-start | bytes 6684672 | tf_op jit(solution)/shard_map/all_gather | solution.py:22
  8.4 129.2 %all-gather.8.cloned.1.call-start = ((), (), s32[]{:S(2)}) async-start(), calls=%async_computation.3 | async-start | bytes 2228224 | tf_op jit(solution)/shard_map/all_gather | solution.py:72
  9.1 13.1 %copy-start.4 = (s32[16]{0:T(128)S(1)}, s32[16]{0:T(128)}, u32[]{:S(2)}) copy-start(s32[16]{0:T(128)} %param.9) | copy-start | bytes 196
  22.2 18.9 %copy-start.3 = (bf16[512,128]{1,0:T(8,128)(2,1)S(1)}, bf16[512,128]{1,0:T(8,128)(2,1)}, u32[]{:S(2)}) copy-start(bf16[512,128]{1,0:T(8,128)(2,1)} %param.13) | copy-start | bytes 393220
  31.0 5.9 %copy-start = (bf16[16,256,2048]{2,1,0:T(8,128)(2,1)}, bf16[16,256,2048]{2,1,0:T(8,128)(2,1)S(1)}, u32[]{:S(2)}) copy-start(bf16[16,256,2048]{2,1,0:T(8,128)(2,1)S(1)} %broadcast_select_fusion) | copy-start | bytes 50331652
  37.0 24.5 %collective-permute-start = (bf16[256,2048]{1,0:T(8,128)(2,1)S(1)}, bf16[256,2048]{1,0:T(8,128)(2,1)S(1)}, u32[]{:S(2)}, u32[]{:S(2)}) collective-permute-start(bf16[256,2048]{1,0:T(8,128)(2,1)S(1)} %slice_bitcast_fusion), channel_id=1, source_target_pairs={{0,8},{8,16},{16,24},{24,32},{32,40},{40,48},{48,56},{56,64},{64,7... | collective-permute-start | bytes 3145736 | tf_op jit(solution)/shard_map/ppermute | solution.py:13
  41.9 160.2 %all-gather.6.cloned.1.call-start = ((), (), s32[]{:S(2)}) async-start(), calls=%async_computation.2 | async-start | bytes 5242880 | tf_op jit(solution)/shard_map/all_gather | solution.py:71
  42.0 2.3 %copy-start.1 = (bf16[1024,2048]{1,0:T(8,128)(2,1)S(1)}, bf16[1024,2048]{1,0:T(8,128)(2,1)}, u32[]{:S(2)}) copy-start(bf16[1024,2048]{1,0:T(8,128)(2,1)} %param.7) | copy-start | bytes 12582916
  42.0 19.5 %slice-start = ((bf16[16,256,2048]{2,1,0:T(8,128)(2,1)}), bf16[15,256,2048]{2,1,0:T(8,128)(2,1)S(1)}, s32[]{:S(2)}) async-start(bf16[16,256,2048]{2,1,0:T(8,128)(2,1)} %copy-done), calls=%async_computation.4 | async-start | bytes 31457280 | tf_op jit(solution)/shard_map/slice | solution.py:55
  120.0 2.0 copy-start.2
Sparse Core Ops, SparseCore 0:
  9.0 46.2 all-gather.3
  57.0 37.4 all-gather.7
  137.7 64.4 all-gather.5
where the time goes:
time: 216 us; the launch traced here: 215 us
  matrix products  55.9 us (26%)
  waiting for transfers between devices  42.7 us (20%)
  local copies, waits for them, and re-layouts  42.7 us (20%)
  blocking collectives  35.9 us (17%)
  other arithmetic  20.2 us (9%)
  between operations  13.2 us (6%)
  starting transfers between devices  4.22 us (2%)
    all_to_all x1, blocking collectives, local(): lax.all_to_all(wide_rows, 'head', split_axis=1, concat_axis=0, tiled=True)  35.9 us
    dot_general x3, matrix products, fold_rows(): return jnp.dot(source, shard_rows, preferred_element_type=jnp.float32)  34.1 us
    all_gather x1, waiting for transfers between devices, local(): every_head = lax.all_gather(attended, 'head', axis=1, tiled=True)  26.3 us
    ppermute x1, waiting for transfers between devices, passed_along(): return lax.ppermute(block, axis, route)  16.4 us
    gather x1, local copies, waits for them, and re-layouts, local(): retrieved = jnp.take(neighbor_bank, slots, axis=0)  13.1 us
    unnamed x12, local copies, waits for them, and re-layouts  12.1 us
    dot_general x1, matrix products, attend(): jnp.einsum('chmn,cnhd->cmhd', weights, value_blocks, preferred_element_ty...  11.9 us
    select_n x2, other arithmetic, local(): retrieved = jnp.take(neighbor_bank, slots, axis=0)  9.4 us
  transfers between devices with their start and end apart: 4, of which 2 were waited for; matrix products, arithmetic and copies ran while one was open for 47% of the time, Pallas kernels for 0%

commit v1 on v0

--- a/solution.py
+++ b/solution.py
@@ -70,7 +70,12 @@
     attended = attend(query_blocks, key_blocks, value_blocks)
     every_head = lax.all_gather(attended, "head", axis=1, tiled=True)
     wide_rows = lax.all_gather(w_out, "seq", axis=1, tiled=True)
-    own_columns = lax.all_to_all(wide_rows, "head", split_axis=1, concat_axis=0, tiled=True)
+    own_columns = jnp.concatenate(
+        lax.all_to_all(
+            jnp.stack(jnp.split(wide_rows, lax.axis_size("head"), axis=1)), "head", 0, 0
+        ),
+        axis=0,
+    )
     return jnp.dot(every_head, own_columns, preferred_element_type=jnp.float32).astype(jnp.bfloat16)
 
 

time: 216 us -> 217 us (level)
    all_to_all x1 -> x0, local copies, waits for them, and re-layouts: 2.36 us -> none  [local(): lax.all_to_all(wide_rows, 'head', split_axis=1, concat_axis=0, tiled=True)]
    unnamed x12 -> x9, local copies, waits for them, and re-layouts: 12.1 us -> 11.3 us
  transfers between devices with their start and end apart: 4 -> 4, of which waited for: 2 -> 2; matrix products, arithmetic and copies ran while one was open for 47% -> 46% of each run, Pallas kernels for 0% -> 0%
where the time goes in v1:
time: 217 us; the launch traced here: 216 us
  matrix products  55.3 us (25%)
  waiting for transfers between devices  44.2 us (20%)
  local copies, waits for them, and re-layouts  41.2 us (19%)
  blocking collectives  37.4 us (17%)
  other arithmetic  20.4 us (9%)
  between operations  13.2 us (6%)
  starting transfers between devices  4.2 us (2%)
    all_to_all x1, blocking collectives, local(): lax.all_to_all(jnp.stack(jnp.split(wide_rows, lax.axis_size('head'), axis...  37.4 us
    dot_general x3, matrix products, fold_rows(): return jnp.dot(source, shard_rows, preferred_element_type=jnp.float32)  34.1 us
    all_gather x1, waiting for transfers between devices, local(): every_head = lax.all_gather(attended, 'head', axis=1, tiled=True)  27 us
    ppermute x1, waiting for transfers between devices, passed_along(): return lax.ppermute(block, axis, route)  17.2 us
    gather x1, local copies, waits for them, and re-layouts, local(): retrieved = jnp.take(neighbor_bank, slots, axis=0)  13.1 us
    dot_general x1, matrix products, attend(): jnp.einsum('chmn,cnhd->cmhd', weights, value_blocks, preferred_element_ty...  11.9 us
    unnamed x9, local copies, waits for them, and re-layouts  11.3 us
    select_n x2, other arithmetic, local(): retrieved = jnp.take(neighbor_bank, slots, axis=0)  9.38 us
  transfers between devices with their start and end apart: 4, of which 2 were waited for; matrix products, arithmetic and copies ran while one was open for 46% of the time, Pallas kernels for 0%

profile of v1, /device:TPU:3, one launch (start us, length us, event | category | flops | bytes accessed | tf_op | source)
XLA Modules:
  0.0 215.9 jit_solution(10270995641923392693)
XLA Ops:
  6.5 1.8 pad_maximum_fusion.2
  8.4 0.0 all-gather.8.cloned.1.call-start
  8.4 0.7 compare_select_fusion
  9.1 13.1 %gather_fusion = bf16[16,256,2048]{2,1,0:T(8,128)(2,1)} fusion(bf16[16,256,2048]{2,1,0:T(8,128)(2,1)} %param.8, s32[1024]{0:T(1024)S(1)} %pad_clamp_fusion), kind=kCustom, calls=%fused_computation | custom fusion | bytes 33554496 | tf_op jit(solution)/shard_map/jit(_take)/gather | solution.py:53
  22.2 8.7 %broadcast_select_fusion = bf16[16,256,2048]{2,1,0:T(8,128)(2,1)S(1)} fusion(bf16[16,256,2048]{2,1,0:T(8,128)(2,1)} %gather_fusion, pred[16]{0:T(512)(128)(4,1)S(1)} %compare_and_fusion), kind=kLoop, calls=%fused_computation.3 | loop fusion | flops 8388608 | bytes 33554448 | tf_op jit(solution)/shard_map/jit(_take)/select_n | solution.py:53
  31.0 5.9 %copy-done = bf16[16,256,2048]{2,1,0:T(8,128)(2,1)} copy-done((bf16[16,256,2048]{2,1,0:T(8,128)(2,1)}, bf16[16,256,2048]{2,1,0:T(8,128)(2,1)S(1)}, u32[]{:S(2)}) %copy-start) | copy-done | bytes 16777240
  36.9 0.1 slice_bitcast_fusion
  36.9 4.1 %collective-permute-start = (bf16[256,2048]{1,0:T(8,128)(2,1)S(1)}, bf16[256,2048]{1,0:T(8,128)(2,1)S(1)}, u32[]{:S(2)}, u32[]{:S(2)}) collective-permute-start(bf16[256,2048]{1,0:T(8,128)(2,1)S(1)} %slice_bitcast_fusion), channel_id=1, source_target_pairs={{0,8},{8,16},{16,24},{24,32},{32,40},{40,48},{48,56},{56,64},{64,7... | collective-permute-start | bytes 3145736 | tf_op jit(solution)/shard_map/ppermute | solution.py:13
  41.1 0.0 all-gather.8.cloned.1.call-update
  41.1 0.0 all-gather.6.cloned.1.call-start
  41.2 2.2 %copy-done.1 = bf16[1024,2048]{1,0:T(8,128)(2,1)S(1)} copy-done((bf16[1024,2048]{1,0:T(8,128)(2,1)S(1)}, bf16[1024,2048]{1,0:T(8,128)(2,1)}, u32[]{:S(2)}) %copy-start.1) | copy-done | bytes 4194328
  43.4 0.9 fusion.1
  44.3 17.2 %collective-permute-done = bf16[256,2048]{1,0:T(8,128)(2,1)S(1)} collective-permute-done((bf16[256,2048]{1,0:T(8,128)(2,1)S(1)}, bf16[256,2048]{1,0:T(8,128)(2,1)S(1)}, u32[]{:S(2)}, u32[]{:S(2)}) %collective-permute-start) | collective-permute-done | bytes 1048608 | tf_op jit(solution)/shard_map/ppermute | solution.py:13
  61.5 6.4 %pad_maximum_fusion = bf16[16,256,2048]{2,1,0:T(8,128)(2,1)} fusion(bf16[15,256,2048]{2,1,0:T(8,128)(2,1)S(1)} %slice-done, bf16[1,256,2048]{2,1,0:T(8,128)(2,1)S(1)} %bitcast.29), kind=kLoop, calls=%fused_computation.2 | loop fusion | flops 8388608 | bytes 33554432 | tf_op jit(solution)/shard_map/concatenate | solution.py:55
  68.0 14.5 %convolution_convert_fusion = bf16[4096,512]{1,0:T(8,128)(2,1)} fusion(bf16[4096,2048]{1,0:T(8,128)(2,1)} %bitcast.24, bf16[2048,1536]{1,0:T(8,128)(2,1)} %all-gather.4.cloned.1.call-done), kind=kOutput, calls=%fused_computation.8 | convolution fusion | flops 8592031744 | bytes 23068672 | tf_op jit(solution)/shard_map/dot_general | solution.py:39
  82.4 6.9 %reshape.36 = bf16[16,256,4,128]{3,2,1,0:T(4,128)(2,1)} reshape(bf16[4096,512]{1,0:T(8,128)(2,1)} %convolution_convert_fusion) | data formatting | bytes 8388608 | tf_op jit(solution)/shard_map/reshape | solution.py:64
  89.3 5.3 %fusion.21 = bf16[1024,512]{1,0:T(8,128)(2,1)S(1)} fusion(bf16[2048,1536]{1,0:T(8,128)(2,1)} %all-gather.4.cloned.1.call-done, bf16[1024,2048]{1,0:T(8,128)(2,1)} %param.7, f32[1024]{0:T(1024)S(1)} %add_rsqrt_fusion), kind=kOutput, calls=%fused_computation.27 | convolution fusion | flops 2154299392 | bytes 7344128 | tf_op jit(solution)/shard_map/dot_general | solution.py:39
  94.6 0.3 reshape.35
  94.9 14.4 %convolution_convert_fusion.1 = bf16[4096,512]{1,0:T(8,128)(2,1)} fusion(bf16[4096,2048]{1,0:T(8,128)(2,1)} %bitcast.25, bf16[2048,1536]{1,0:T(8,128)(2,1)} %all-gather.4.cloned.1.call-done), kind=kOutput, calls=%fused_computation.9 | convolution fusion | flops 8592031744 | bytes 23068672 | tf_op jit(solution)/shard_map/dot_general | solution.py:39
  109.3 6.9 %reshape.34 = bf16[16,256,4,128]{3,2,1,0:T(4,128)(2,1)} reshape(bf16[4096,512]{1,0:T(8,128)(2,1)} %convolution_convert_fusion.1) | data formatting | bytes 8388608 | tf_op jit(solution)/shard_map/reshape | solution.py:67
  116.2 3.8 %fusion.7 = f32[16,4,64,256]{3,2,1,0:T(8,128)S(1)} fusion(bf16[16,256,4,128]{3,2,1,0:T(4,128)(2,1)} %reshape.36, bf16[16,64,4,128]{3,2,1,0:T(4,128)(2,1)S(1)} %reshape.35), kind=kOutput, calls=%fused_computation.13 | convolution fusion | flops 268435456 | bytes 9437184 | tf_op jit(solution)/shard_map/cmhd,cnhd->chmn/dot_general | solution.py:26
  119.9 2.0 copy-done.2
  121.9 1.6 fusion.38
  123.5 11.9 %fusion.26 = bf16[16,64,4,128]{3,1,2,0:T(8,128)(2,1)S(1)} fusion(bf16[16,256,4,128]{3,2,1,0:T(4,128)(2,1)} %reshape.34, f32[16,4,64]{2,1,0:T(4,128)S(1)} %fusion.38, f32[16,4,64,256]{3,2,1,0:T(8,128)} %copy-done.2), kind=kOutput, calls=%fused_computation.29 | convolution fusion | flops 274206976 | bytes 9453568 | tf_op jit(solution)/shard_map/chmn,cnhd->cmhd/dot_general | solution.py:32
  135.5 0.9 copy.14
  136.4 1.2 copy.27
  137.5 0.0 all-gather.8.cloned.1.call-done
  137.6 1.7 slice_bitcast_fusion.4
  139.2 0.3 pad_maximum_fusion.1
  139.5 37.4 %all_to_all.5 = bf16[4,512,512]{2,1,0:T(8,128)(2,1)S(1)} all-to-all(bf16[4,512,512]{2,1,0:T(8,128)(2,1)S(1)} %pad_maximum_fusion.1), channel_id=1, replica_groups=mesh['seq'=16,'head'=4,'batch'=2] {'head'}, dimensions={0} | all-to-all | bytes 4194304 | tf_op jit(solution)/shard_map/all_to_all | solution.py:74
  176.9 27.0 %all-gather.6.cloned.1.call-done = bf16[1024,2048]{1,0:T(8,128)(2,1)} async-done(((bf16[1024,512]{1,0:T(8,128)(2,1)}), bf16[1024,2048]{1,0:T(8,128)(2,1)}) %all-gather.6.cloned.1.call-update) | async-done | bytes 4194320 | tf_op jit(solution)/shard_map/all_gather | solution.py:71
  203.9 5.5 %convolution_convert_fusion.2 = bf16[1024,512]{1,0:T(8,128)(2,1)} fusion(bf16[1024,2048]{1,0:T(8,128)(2,1)} %all-gather.6.cloned.1.call-done, bf16[2048,512]{1,0:T(8,128)(2,1)S(1)} %bitcast.28), kind=kOutput, calls=%fused_computation.28 | convolution fusion | flops 2148007936 | bytes 7340032 | tf_op jit(solution)/shard_map/dot_general | solution.py:79
  (14 shorter events, 0.1 us)
Async XLA Ops:
  6.5 61.4 %all-gather.4.cloned.1.call-start = ((), (), s32[]{:S(2)}) async-start(), calls=%async_computation.1 | async-start | bytes 6684672 | tf_op jit(solution)/shard_map/all_gather | solution.py:22
  8.4 129.2 %all-gather.8.cloned.1.call-start = ((), (), s32[]{:S(2)}) async-start(), calls=%async_computation.3 | async-start | bytes 2228224 | tf_op jit(solution)/shard_map/all_gather | solution.py:72
  9.1 13.1 %copy-start.3 = (s32[16]{0:T(128)S(1)}, s32[16]{0:T(128)}, u32[]{:S(2)}) copy-start(s32[16]{0:T(128)} %param.9) | copy-start | bytes 196
  31.0 5.9 %copy-start = (bf16[16,256,2048]{2,1,0:T(8,128)(2,1)}, bf16[16,256,2048]{2,1,0:T(8,128)(2,1)S(1)}, u32[]{:S(2)}) copy-start(bf16[16,256,2048]{2,1,0:T(8,128)(2,1)S(1)} %broadcast_select_fusion) | copy-start | bytes 50331652
  36.9 24.6 %collective-permute-start = (bf16[256,2048]{1,0:T(8,128)(2,1)S(1)}, bf16[256,2048]{1,0:T(8,128)(2,1)S(1)}, u32[]{:S(2)}, u32[]{:S(2)}) collective-permute-start(bf16[256,2048]{1,0:T(8,128)(2,1)S(1)} %slice_bitcast_fusion), channel_id=1, source_target_pairs={{0,8},{8,16},{16,24},{24,32},{32,40},{40,48},{48,56},{56,64},{64,7... | collective-permute-start | bytes 3145736 | tf_op jit(solution)/shard_map/ppermute | solution.py:13
  41.1 162.8 %all-gather.6.cloned.1.call-start = ((), (), s32[]{:S(2)}) async-start(), calls=%async_computation.2 | async-start | bytes 5242880 | tf_op jit(solution)/shard_map/all_gather | solution.py:71
  41.1 2.3 %copy-start.1 = (bf16[1024,2048]{1,0:T(8,128)(2,1)S(1)}, bf16[1024,2048]{1,0:T(8,128)(2,1)}, u32[]{:S(2)}) copy-start(bf16[1024,2048]{1,0:T(8,128)(2,1)} %param.7) | copy-start | bytes 12582916
  41.2 20.4 %slice-start = ((bf16[16,256,2048]{2,1,0:T(8,128)(2,1)}), bf16[15,256,2048]{2,1,0:T(8,128)(2,1)S(1)}, s32[]{:S(2)}) async-start(bf16[16,256,2048]{2,1,0:T(8,128)(2,1)} %copy-done), calls=%async_computation.4 | async-start | bytes 31457280 | tf_op jit(solution)/shard_map/slice | solution.py:55
  119.9 2.0 copy-start.2
Sparse Core Ops, SparseCore 0:
  9.0 46.2 all-gather.3
  56.9 40.4 all-gather.7
  137.7 66.1 all-gather.5
